TPU v7x, 32 devices: a whole 2x2x4 slice. The times are simulated.
32 devices in a mesh: gx: 8 (over z, x), gy: 4 (over y, core).
Axes of the slice: x: 2, y: 2, z: 4, core: 2. Of those that a mesh axis runs over, the one named last changes fastest.
Arguments:
- gradient: float32 [1024, 128], P('gx', 'gy'), may hold values from -6 to 6
- stat_old: float32 [1024, 1024], P('gx', 'gy'), may hold values from -1.001 to 1.001, as said below
Outputs:
- statistic: float32 [1024, 1024], P('gx', 'gy')
- inverse_root: float32 [1024, 1024], P('gx', 'gy')
Inputs may be any that keep to these rules, and one draw needn't show every extreme that they name: stat_old is symmetric positive semidefinite with unit diagonal, the Gram matrix of 1024 unit-length rows of 256 entries.
All inputs are finite; a program needn't handle non-finite values.
Results may differ from a plain program's by a relative error of at most 0.0003.
Values sent between devices are 32-bit elements.
A program may use at most 64 MiB of HBM per device.

v0:
```python
import jax
import jax.numpy as jnp
from jax import lax
from jax.sharding import PartitionSpec as P


def folded(shard, axis, dim, absorb, state):
    everything = jax.tree.map(lambda a: lax.all_gather(a, axis, axis=dim, tiled=True), shard)
    return absorb(state, everything, jnp.int32(0))


def spread(block, axis, owner):
    block = jnp.where(lax.axis_index(axis) == owner, block, jnp.zeros_like(block))
    return lax.psum(block, axis)


def matmul(leading, trailing):
    return jnp.dot(
        leading, trailing, preferred_element_type=jnp.float32, precision=lax.Precision.HIGHEST
    )


def panels(factor_one, factor_two):
    whole_row = lax.all_gather(factor_one, "gy", axis=1, tiled=True)

    def accumulate(running, shard_rows, first_row):
        matching = lax.dynamic_slice_in_dim(whole_row, first_row, shard_rows.shape[0], 1)
        return running + matmul(matching, shard_rows)

    empty = jnp.zeros((factor_one.shape[0], factor_two.shape[1]), jnp.float32)
    return folded(factor_two, "gx", 0, accumulate, empty)


def product(factor_one, factor_two):
    return panels(factor_one, factor_two)


def local(gradient, stat_old):
    count_rows = lax.axis_size("gx")
    count_cols = lax.axis_size("gy")
    factor = count_rows // count_cols
    piece_width = stat_old.shape[0]
    row_index = lax.axis_index("gx")
    col_index = lax.axis_index("gy")
    panel_rows = lax.all_gather(gradient, "gy", axis=1, tiled=True)
    outer_parts = []
    for member in range(factor):
        column_rows = spread(panel_rows, "gx", col_index * factor + member)
        outer_parts.append(matmul(panel_rows, column_rows.T))
    outer = jnp.concatenate(outer_parts, axis=1) / panel_rows.shape[1]
    statistic = 0.9 * stat_old + outer
    squares = lax.psum(jnp.sum(statistic * statistic), ("gx", "gy"))
    divisor = 2.0 * jnp.sqrt(squares / (piece_width * count_rows))
    global_rows = row_index * piece_width + lax.broadcasted_iota(jnp.int32, stat_old.shape, 0)
    global_cols = col_index * (factor * piece_width) + lax.broadcasted_iota(
        jnp.int32, stat_old.shape, 1
    )
    identity = (global_rows == global_cols).astype(jnp.float32)
    normed = statistic / divisor
    first_step = 1.5 * identity - 0.5 * normed
    root_half = product(normed, first_step)
    product_mid = product(first_step, root_half)
    second_step = 1.5 * identity - 0.5 * product_mid
    inverse_root = product(second_step, first_step)
    return (statistic, inverse_root)


def solution(mesh):
    return jax.shard_map(
        local,
        mesh=mesh,
        in_specs=(P("gx", "gy"), P("gx", "gy")),
        out_specs=(P("gx", "gy"), P("gx", "gy")),
        check_vma=False,
    )
```

profile of v0, /device:TPU:0, one launch (start us, length us, event | category | flops | bytes accessed | tf_op | source)
XLA Modules:
  0.0 230.7 jit_solution(9310152714000626148)
XLA Ops:
  7.2 0.0 all-reduce.3.cloned.1.call-start
  7.2 0.6 copy-done.4
  7.9 6.2 %all_gather.19 = f32[128,128]{0,1:T(8,128)S(1)} all-gather(f32[128,32]{0,1:T(8,128)S(1)} %copy-done.4), channel_id=1, replica_groups=mesh['gx'=8,'gy'=4] {'gy'}, dimensions={1}, use_global_device_ids=true | all-gather | bytes 81920 | tf_op jit(solution)/shard_map/all_gather | solution.py:45
  14.1 0.7 broadcast_select_fusion.1
  14.8 0.0 all-gather.3.cloned.1.call-start
  14.8 0.2 copy-done.2
  15.0 0.1 copy.4
  15.1 72.2 %all-reduce.3.cloned.1.call-done = (f32[128,128]{0,1:T(8,128)}, f32[128,128]{0,1:T(8,128)}) async-done(((f32[128,128]{0,1:T(8,128)}, f32[128,128]{0,1:T(8,128)}), (f32[128,128]{0,1:T(8,128)}, f32[128,128]{0,1:T(8,128)})) %all-reduce.3.cloned.1.call-update) | async-done | bytes 131088 | tf_op jit(solution)/shard_map/psum | solution.py:14
  87.4 1.2 convolution_bitcast_fusion
  88.6 0.3 convolution_bitcast_fusion.1
  88.8 0.6 multiply_reduce_fusion
  89.5 39.6 %psum.23 = f32[]{:T(128)} all-reduce(f32[]{:T(128)} %get-tuple-element.8), channel_id=1, replica_groups=mesh['gx'=8,'gy'=4] {'gx','gy'}, use_global_device_ids=true, to_apply=%region_3.4 | all-reduce | flops 1 | bytes 8 | tf_op jit(solution)/shard_map/psum | solution.py:52
  129.8 0.8 select_subtract_fusion
  130.5 0.0 all-gather.5.cloned.1.call-start
  130.6 8.1 %all_gather.21 = f32[128,1024]{0,1:T(8,128)S(1)} all-gather(f32[128,256]{0,1:T(8,128)S(1)} %get-tuple-element.7), channel_id=1, replica_groups=mesh['gx'=8,'gy'=4] {'gy'}, dimensions={1}, use_global_device_ids=true | all-gather | bytes 655360 | tf_op jit(solution)/shard_map/all_gather | solution.py:24
  138.7 31.3 %all-gather.3.cloned.1.call-done = f32[1024,256]{0,1:T(8,128)} async-done(((f32[128,256]{0,1:T(8,128)}), f32[1024,256]{0,1:T(8,128)}) %all-gather.3.cloned.1.call-update) | async-done | bytes 1048592 | tf_op jit(solution)/shard_map/all_gather | solution.py:8
  170.0 2.9 %fusion.3 = f32[128,256]{1,0:T(8,128)} fusion(f32[128,1024]{0,1:T(8,128)S(1)} %all_gather.21, f32[1024,256]{0,1:T(8,128)} %all-gather.3.cloned.1.call-done), kind=kOutput, calls=%fused_computation.13 | convolution fusion | flops 402653184 | bytes 1703936 | tf_op jit(solution)/shard_map/dot_general | solution.py:18
  172.9 0.8 copy.5
  173.7 0.1 copy-done.1
  173.8 7.3 %all_gather.20 = f32[128,1024]{0,1:T(8,128)S(1)} all-gather(f32[128,256]{0,1:T(8,128)S(1)} %copy-done.1), channel_id=1, replica_groups=mesh['gx'=8,'gy'=4] {'gy'}, dimensions={1}, use_global_device_ids=true | all-gather | bytes 655360 | tf_op jit(solution)/shard_map/all_gather | solution.py:24
  181.1 31.3 %all-gather.5.cloned.1.call-done = f32[1024,256]{1,0:T(8,128)} async-done(((f32[128,256]{1,0:T(8,128)}), f32[1024,256]{1,0:T(8,128)}) %all-gather.5.cloned.1.call-update) | async-done | bytes 1048592 | tf_op jit(solution)/shard_map/all_gather | solution.py:8
  212.4 3.0 %fusion = f32[128,256]{0,1:T(8,128)S(1)} fusion(f32[128,1024]{0,1:T(8,128)S(1)} %all_gather.20, f32[1024,256]{1,0:T(8,128)} %all-gather.5.cloned.1.call-done, s32[128]{0:T(128)S(1)} %iota_add_fusion.1, s32[256]{0:T(256)S(1)} %iota_add_fusion), kind=kOutput, calls=%fused_computation.1 | convolution fusion | flops 402784256 | bytes 1705472 | tf_op jit(solution)/shard_map/dot_general | solution.py:18
  215.4 7.2 %all_gather.24 = f32[128,1024]{0,1:T(8,128)S(1)} all-gather(f32[128,256]{0,1:T(8,128)S(1)} %fusion), channel_id=1, replica_groups=mesh['gx'=8,'gy'=4] {'gy'}, dimensions={1}, use_global_device_ids=true | all-gather | bytes 655360 | tf_op jit(solution)/shard_map/all_gather | solution.py:24
  222.5 1.7 fusion.4
  (12 shorter events, 0.1 us)
Async XLA Ops:
  7.2 0.7 copy-start.4
  7.2 80.2 %all-reduce.3.cloned.1.call-start = ((), (), s32[]{:S(2)}) async-start(), calls=%async_computation.2 | async-start | bytes 262144 | tf_op jit(solution)/shard_map/psum | solution.py:14
  14.1 1.0 copy-start.2
  14.8 155.2 %all-gather.3.cloned.1.call-start = ((), (), s32[]{:S(2)}) async-start(), calls=%async_computation | async-start | bytes 1179648 | tf_op jit(solution)/shard_map/all_gather | solution.py:8
  87.4 1.2 copy-start.3
  130.5 81.8 %all-gather.5.cloned.1.call-start = ((), (), s32[]{:S(2)}) async-start(), calls=%async_computation.1 | async-start | bytes 1179648 | tf_op jit(solution)/shard_map/all_gather | solution.py:8
  172.9 0.9 copy-start.1
  181.1 41.5 %copy-start = (f32[1024,256]{0,1:T(8,128)S(1)}, f32[1024,256]{0,1:T(8,128)}, u32[]{:S(2)}) copy-start(f32[1024,256]{0,1:T(8,128)} %all-gather.3.cloned.1.call-done) | copy-start | bytes 3145732
Sparse Core Ops, SparseCore 0:
  14.9 72.4 all-reduce.2
  130.7 39.2 all-gather.2
  173.0 39.2 all-gather.4
where the time goes:
time: 231 us
  waiting for transfers between devices  135 us (58%)
  blocking collectives  68.3 us (30%)
  between operations  14.5 us (6%)
  matrix products  9 us (4%)
    psum x1, waiting for transfers between devices, spread(): return lax.psum(block, axis)  72.2 us
    all_gather x2, waiting for transfers between devices, folded(): lax.all_gather(a, axis, axis=dim, tiled=True)  62.5 us
    psum x1, blocking collectives, local(): squares = lax.psum(jnp.sum(statistic * statistic), ('gx', 'gy'))  39.6 us
    all_gather x3, blocking collectives, panels(): whole_row = lax.all_gather(factor_one, 'gy', axis=1, tiled=True)  22.6 us
    dot_general x5, matrix products, matmul(): jnp.dot(leading, trailing, preferred_element_type=jnp.float32, precision=...  9 us
    all_gather x1, blocking collectives, local(): panel_rows = lax.all_gather(gradient, 'gy', axis=1, tiled=True)  6.2 us
  transfers between devices with their start and end apart: 3, of which 3 were waited for; matrix products, arithmetic and copies ran while one was open for 0% of the time, Pallas kernels for 0%

commit v1 on v0

--- a/solution.py
+++ b/solution.py
@@ -11,7 +11,7 @@
 
 def spread(block, axis, owner):
     block = jnp.where(lax.axis_index(axis) == owner, block, jnp.zeros_like(block))
-    return lax.psum(block, axis)
+    return jnp.sum(lax.all_gather(block, axis), axis=0)
 
 
 def matmul(leading, trailing):

time: 231 us -> 223 us (0.965)
  waiting for transfers between devices: 135 us -> 63.3 us
  blocking collectives: 68.3 us -> 132 us
    psum x1 -> x0, waiting for transfers between devices: 72.2 us -> none  [spread(): return lax.psum(block, axis)]
    all_gather x0 -> x2, blocking collectives: none -> 63.5 us  [spread(): return jnp.sum(lax.all_gather(block, axis), axis=0)]
  transfers between devices with their start and end apart: 3 -> 2, of which waited for: 3 -> 2; matrix products, arithmetic and copies ran while one was open for 0% -> 0% of each run, Pallas kernels for 0% -> 0%
where the time goes in v1:
time: 223 us
  blocking collectives  132 us (59%)
  waiting for transfers between devices  63.3 us (28%)
  between operations  14.8 us (7%)
  matrix products  8.15 us (4%)
  local copies, waits for them, and re-layouts  2.71 us (1%)
    all_gather x2, blocking collectives, spread(): return jnp.sum(lax.all_gather(block, axis), axis=0)  63.5 us
    all_gather x2, waiting for transfers between devices, folded(): lax.all_gather(a, axis, axis=dim, tiled=True)  63.2 us
    psum x1, blocking collectives, local(): squares = lax.psum(jnp.sum(statistic * statistic), ('gx', 'gy'))  40 us
    all_gather x3, blocking collectives, panels(): whole_row = lax.all_gather(factor_one, 'gy', axis=1, tiled=True)  22.6 us
    dot_general x5, matrix products, matmul(): jnp.dot(leading, trailing, preferred_element_type=jnp.float32, precision=...  8.15 us
    all_gather x1, blocking collectives, local(): panel_rows = lax.all_gather(gradient, 'gy', axis=1, tiled=True)  6.2 us
  transfers between devices with their start and end apart: 2, of which 2 were waited for; matrix products, arithmetic and copies ran while one was open for 0% of the time, Pallas kernels for 0%

profile of v1, /device:TPU:0, one launch (start us, length us, event | category | flops | bytes accessed | tf_op | source)
XLA Modules:
  0.0 223.0 jit_solution(18123898331182313358)
XLA Ops:
  7.3 0.6 copy-done.2
  7.9 6.2 %all_gather.31 = f32[128,128]{0,1:T(8,128)S(1)} all-gather(f32[128,32]{0,1:T(8,128)S(1)} %copy-done.2), channel_id=1, replica_groups=mesh['gx'=8,'gy'=4] {'gy'}, dimensions={1}, use_global_device_ids=true | all-gather | bytes 81920 | tf_op jit(solution)/shard_map/all_gather | solution.py:45
  14.1 1.0 copy.6
  15.1 32.4 %all-gather = f32[1024,128]{0,1:T(8,128)S(1)} all-gather(f32[128,128]{0,1:T(8,128)S(1)} %get-tuple-element.10), channel_id=2, replica_groups=mesh['gx'=8,'gy'=4] {'gx'}, dimensions={0}, use_global_device_ids=true | all-gather | bytes 589824 | tf_op jit(solution)/shard_map/all_gather | solution.py:14
  47.5 0.1 copy.8
  47.6 0.1 bitcast_reduce_fusion.1
  47.7 0.3 convolution_bitcast_fusion.1
  48.0 31.2 %all-gather.1 = f32[1024,128]{0,1:T(8,128)S(1)} all-gather(f32[128,128]{0,1:T(8,128)S(1)} %get-tuple-element.11), channel_id=3, replica_groups=mesh['gx'=8,'gy'=4] {'gx'}, dimensions={0}, use_global_device_ids=true | all-gather | bytes 589824 | tf_op jit(solution)/shard_map/all_gather | solution.py:14
  79.2 0.1 copy.9
  79.3 0.1 bitcast_reduce_fusion
  79.4 0.3 convolution_bitcast_fusion
  79.7 0.6 multiply_reduce_fusion
  80.3 40.0 %psum.7 = f32[]{:T(128)} all-reduce(f32[]{:T(128)} %get-tuple-element.8), channel_id=1, replica_groups=mesh['gx'=8,'gy'=4] {'gx','gy'}, use_global_device_ids=true, to_apply=%region_3.4 | all-reduce | flops 1 | bytes 8 | tf_op jit(solution)/shard_map/psum | solution.py:52
  121.0 0.8 select_subtract_fusion
  121.8 8.1 %all_gather.37 = f32[128,1024]{0,1:T(8,128)S(1)} all-gather(f32[128,256]{0,1:T(8,128)S(1)} %get-tuple-element.7), channel_id=1, replica_groups=mesh['gx'=8,'gy'=4] {'gy'}, dimensions={1}, use_global_device_ids=true | all-gather | bytes 655360 | tf_op jit(solution)/shard_map/all_gather | solution.py:24
  130.0 32.0 %all-gather.5.cloned.1.call-done = f32[1024,256]{0,1:T(8,128)} async-done(((f32[128,256]{0,1:T(8,128)}), f32[1024,256]{0,1:T(8,128)}) %all-gather.5.cloned.1.call-update) | async-done | bytes 1048592 | tf_op jit(solution)/shard_map/all_gather | solution.py:8
  161.9 2.9 %fusion.3 = f32[128,256]{1,0:T(8,128)} fusion(f32[128,1024]{0,1:T(8,128)S(1)} %all_gather.37, f32[1024,256]{0,1:T(8,128)} %all-gather.5.cloned.1.call-done), kind=kOutput, calls=%fused_computation.15 | convolution fusion | flops 402653184 | bytes 1703936 | tf_op jit(solution)/shard_map/dot_general | solution.py:18
  164.9 0.8 copy.7
  165.6 0.1 copy-done.1
  165.8 7.3 %all_gather.36 = f32[128,1024]{0,1:T(8,128)S(1)} all-gather(f32[128,256]{0,1:T(8,128)S(1)} %copy-done.1), channel_id=1, replica_groups=mesh['gx'=8,'gy'=4] {'gy'}, dimensions={1}, use_global_device_ids=true | all-gather | bytes 655360 | tf_op jit(solution)/shard_map/all_gather | solution.py:24
  173.0 31.3 %all-gather.7.cloned.1.call-done = f32[1024,256]{1,0:T(8,128)} async-done(((f32[128,256]{1,0:T(8,128)}), f32[1024,256]{1,0:T(8,128)}) %all-gather.7.cloned.1.call-update) | async-done | bytes 1048592 | tf_op jit(solution)/shard_map/all_gather | solution.py:8
  204.3 3.0 %fusion = f32[128,256]{0,1:T(8,128)S(1)} fusion(f32[128,1024]{0,1:T(8,128)S(1)} %all_gather.36, f32[1024,256]{1,0:T(8,128)} %all-gather.7.cloned.1.call-done, s32[128]{0:T(128)S(1)} %iota_add_fusion.1, s32[256]{0:T(256)S(1)} %iota_add_fusion), kind=kOutput, calls=%fused_computation.1 | convolution fusion | flops 402784256 | bytes 1705472 | tf_op jit(solution)/shard_map/dot_general | solution.py:18
  207.3 7.2 %all_gather.40 = f32[128,1024]{0,1:T(8,128)S(1)} all-gather(f32[128,256]{0,1:T(8,128)S(1)} %fusion), channel_id=1, replica_groups=mesh['gx'=8,'gy'=4] {'gy'}, dimensions={1}, use_global_device_ids=true | all-gather | bytes 655360 | tf_op jit(solution)/shard_map/all_gather | solution.py:24
  214.5 1.7 fusion.4
  (11 shorter events, 0.2 us)
Async XLA Ops:
  7.2 0.7 copy-start.2
  7.2 154.8 %all-gather.5.cloned.1.call-start = ((), (), s32[]{:S(2)}) async-start(), calls=%async_computation | async-start | bytes 1179648 | tf_op jit(solution)/shard_map/all_gather | solution.py:8
  121.8 82.5 %all-gather.7.cloned.1.call-start = ((), (), s32[]{:S(2)}) async-start(), calls=%async_computation.1 | async-start | bytes 1179648 | tf_op jit(solution)/shard_map/all_gather | solution.py:8
  164.9 0.9 copy-start.1
  173.0 41.5 %copy-start = (f32[1024,256]{0,1:T(8,128)S(1)}, f32[1024,256]{0,1:T(8,128)}, u32[]{:S(2)}) copy-start(f32[1024,256]{0,1:T(8,128)} %all-gather.5.cloned.1.call-done) | copy-start | bytes 3145732
Sparse Core Ops, SparseCore 0:
  121.9 39.9 all-gather.4
  165.0 39.2 all-gather.6

commit v2 on v0

--- a/solution.py
+++ b/solution.py
@@ -21,7 +21,7 @@
 
 
 def panels(factor_one, factor_two):
-    whole_row = lax.all_gather(factor_one, "gy", axis=1, tiled=True)
+    whole_row = jnp.concatenate(lax.all_gather(factor_one, "gy"), axis=1)
 
     def accumulate(running, shard_rows, first_row):
         matching = lax.dynamic_slice_in_dim(whole_row, first_row, shard_rows.shape[0], 1)

time: 231 us -> 231 us (level)
  no operation moved by 1% of the time
where the time goes in v2:
time: 231 us; the launch traced here: 230 us
  waiting for transfers between devices  135 us (58%)
  blocking collectives  68.7 us (30%)
  between operations  14.5 us (6%)
  matrix products  9.01 us (4%)
    psum x1, waiting for transfers between devices, spread(): return lax.psum(block, axis)  72.2 us
    all_gather x2, waiting for transfers between devices, folded(): lax.all_gather(a, axis, axis=dim, tiled=True)  62.5 us
    psum x1, blocking collectives, local(): squares = lax.psum(jnp.sum(statistic * statistic), ('gx', 'gy'))  39.6 us
    all_gather x3, blocking collectives, panels(): whole_row = jnp.concatenate(lax.all_gather(factor_one, 'gy'), axis=1)  22.7 us
    dot_general x5, matrix products, matmul(): jnp.dot(leading, trailing, preferred_element_type=jnp.float32, precision=...  9.01 us
    all_gather x1, blocking collectives, local(): panel_rows = lax.all_gather(gradient, 'gy', axis=1, tiled=True)  6.48 us
  transfers between devices with their start and end apart: 3, of which 3 were waited for; matrix products, arithmetic and copies ran while one was open for 0% of the time, Pallas kernels for 0%

profile of v2, /device:TPU:0, one launch (start us, length us, event | category | flops | bytes accessed | tf_op | source)
XLA Modules:
  0.0 230.5 jit_solution(4890473471099135862)
XLA Ops:
  7.2 0.0 all-reduce.3.cloned.1.call-start
  7.2 6.5 %all_gather.28 = f32[128,128]{0,1:T(8,128)S(1)} all-gather(f32[128,32]{0,1:T(8,128)} %param.2), channel_id=1, replica_groups=mesh['gx'=8,'gy'=4] {'gy'}, dimensions={1}, use_global_device_ids=true | all-gather | bytes 81920 | tf_op jit(solution)/shard_map/all_gather | solution.py:45
  13.7 0.7 broadcast_select_fusion.1
  14.4 0.0 all-reduce.3.cloned.1.call-update
  14.4 0.0 all-gather.6.cloned.1.call-start
  14.5 0.2 copy-done.2
  14.6 0.1 copy.7
  14.8 72.2 %all-reduce.3.cloned.1.call-done = (f32[128,128]{0,1:T(8,128)}, f32[128,128]{0,1:T(8,128)}) async-done(((f32[128,128]{0,1:T(8,128)}, f32[128,128]{0,1:T(8,128)}), (f32[128,128]{0,1:T(8,128)}, f32[128,128]{0,1:T(8,128)})) %all-reduce.3.cloned.1.call-update) | async-done | bytes 131088 | tf_op jit(solution)/shard_map/psum | solution.py:14
  87.0 1.2 convolution_bitcast_fusion
  88.1 0.3 convolution_bitcast_fusion.1
  88.4 0.6 multiply_reduce_fusion
  89.1 39.6 %psum.23 = f32[]{:T(128)} all-reduce(f32[]{:T(128)} %get-tuple-element.10), channel_id=1, replica_groups=mesh['gx'=8,'gy'=4] {'gx','gy'}, use_global_device_ids=true, to_apply=%region_3.4 | all-reduce | flops 1 | bytes 8 | tf_op jit(solution)/shard_map/psum | solution.py:52
  129.3 0.8 select_subtract_fusion
  130.1 0.0 all-gather.8.cloned.1.call-start
  130.2 8.1 %all-gather.1 = f32[512,256]{0,1:T(8,128)S(1)} all-gather(f32[128,256]{0,1:T(8,128)S(1)} %get-tuple-element.9), channel_id=3, replica_groups=mesh['gx'=8,'gy'=4] {'gy'}, dimensions={0}, use_global_device_ids=true | all-gather | bytes 655360 | tf_op jit(solution)/shard_map/all_gather | solution.py:24
  138.3 31.2 %all-gather.6.cloned.1.call-done = f32[1024,256]{0,1:T(8,128)} async-done(((f32[128,256]{0,1:T(8,128)}), f32[1024,256]{0,1:T(8,128)}) %all-gather.6.cloned.1.call-update) | async-done | bytes 1048592 | tf_op jit(solution)/shard_map/all_gather | solution.py:8
  169.6 2.9 %fusion.3 = f32[128,256]{1,0:T(8,128)} fusion(f32[128,1024]{0,1:T(8,128)S(1)} %bitcast.39, f32[1024,256]{0,1:T(8,128)} %all-gather.6.cloned.1.call-done), kind=kOutput, calls=%fused_computation.16 | convolution fusion | flops 402653184 | bytes 1703936 | tf_op jit(solution)/shard_map/dot_general | solution.py:18
  172.5 0.8 copy.12
  173.2 0.1 copy-done.1
  173.4 7.3 %all-gather = f32[512,256]{0,1:T(8,128)S(1)} all-gather(f32[128,256]{0,1:T(8,128)S(1)} %copy-done.1), channel_id=2, replica_groups=mesh['gx'=8,'gy'=4] {'gy'}, dimensions={0}, use_global_device_ids=true | all-gather | bytes 655360 | tf_op jit(solution)/shard_map/all_gather | solution.py:24
  180.7 31.2 %all-gather.8.cloned.1.call-done = f32[1024,256]{1,0:T(8,128)} async-done(((f32[128,256]{1,0:T(8,128)}), f32[1024,256]{1,0:T(8,128)}) %all-gather.8.cloned.1.call-update) | async-done | bytes 1048592 | tf_op jit(solution)/shard_map/all_gather | solution.py:8
  211.9 3.0 %fusion = f32[128,256]{0,1:T(8,128)S(1)} fusion(f32[128,1024]{0,1:T(8,128)S(1)} %bitcast.38, f32[1024,256]{1,0:T(8,128)} %all-gather.8.cloned.1.call-done, s32[128]{0:T(128)S(1)} %iota_add_fusion.1, s32[256]{0:T(256)S(1)} %iota_add_fusion), kind=kOutput, calls=%fused_computation.1 | convolution fusion | flops 402784256 | bytes 1705472 | tf_op jit(solution)/shard_map/dot_general | solution.py:18
  215.0 7.3 %all-gather.2 = f32[512,256]{0,1:T(8,128)S(1)} all-gather(f32[128,256]{0,1:T(8,128)S(1)} %fusion), channel_id=4, replica_groups=mesh['gx'=8,'gy'=4] {'gy'}, dimensions={0}, use_global_device_ids=true | all-gather | bytes 655360 | tf_op jit(solution)/shard_map/all_gather | solution.py:24
  222.3 1.7 fusion.4
  (13 shorter events, 0.2 us)
Async XLA Ops:
  7.2 79.8 %all-reduce.3.cloned.1.call-start = ((), (), s32[]{:S(2)}) async-start(), calls=%async_computation.2 | async-start | bytes 262144 | tf_op jit(solution)/shard_map/psum | solution.py:14
  13.7 1.0 copy-start.2
  14.4 155.2 %all-gather.6.cloned.1.call-start = ((), (), s32[]{:S(2)}) async-start(), calls=%async_computation | async-start | bytes 1179648 | tf_op jit(solution)/shard_map/all_gather | solution.py:8
  87.0 1.2 copy-start.3
  130.1 81.8 %all-gather.8.cloned.1.call-start = ((), (), s32[]{:S(2)}) async-start(), calls=%async_computation.1 | async-start | bytes 1179648 | tf_op jit(solution)/shard_map/all_gather | solution.py:8
  172.5 0.9 copy-start.1
  214.9 7.3 %copy-start = (f32[1024,256]{0,1:T(8,128)S(1)}, f32[1024,256]{0,1:T(8,128)}, u32[]{:S(2)}) copy-start(f32[1024,256]{0,1:T(8,128)} %all-gather.6.cloned.1.call-done) | copy-start | bytes 3145732
Sparse Core Ops, SparseCore 0:
  14.5 72.4 all-reduce.2
  130.2 39.2 all-gather.5
  172.6 39.2 all-gather.7
